TPU v7x, 32 devices: a whole 2x2x4 slice. The times are simulated.
32 devices in a mesh: section: 4 (over y, core), mp: 8 (over z, x).
Axes of the slice: x: 2, y: 2, z: 4, core: 2. Of those that a mesh axis runs over, the one named last changes fastest.
Arguments:
- arriving: bfloat16 [4, 768, 8192], P('section', None, 'mp'), may hold values from -6 to 6
- norm_gain: bfloat16 [4, 8192], P('section'), may hold values from 0.099609375 to 1.8984375
- w_query: bfloat16 [4, 2048, 8192], P('section', 'mp'), may hold values from -26 to 26
- w_key: bfloat16 [4, 1024, 8192], P('section', 'mp'), may hold values from -1 to 1
- w_value: bfloat16 [4, 1024, 8192], P('section', 'mp'), may hold values from -0.25 to 0.25
- w_out: bfloat16 [4, 2048, 8192], P('section', 'mp'), may hold values from -0.125 to 0.125
Outputs:
- attended: bfloat16 [4, 768, 8192], P('section', 'mp')
- stream_next: bfloat16 [4, 768, 8192], P('section', 'mp')
All inputs are finite; a program needn't handle non-finite values.
Results may differ from a plain program's by a relative error of at most 0.017.
Values may be sent and summed in bfloat16 or wider, within the bound.
A program may use at most 128 MiB of HBM per device.

v0:
```python
import math

import jax
import jax.numpy as jnp
from jax import lax
from jax.sharding import PartitionSpec as P

HD = 128
KV_HEADS = 8


rope_base = 500000.0
norm_eps = 1e-05


def shifted(block, axis, distance):
    devices = range(lax.axis_size(axis))
    route = [((i - distance) % len(devices), i) for i in devices]
    return lax.ppermute(block, axis, route)


def rotate_pairs(channel_major, pair_ids):
    channels = channel_major.shape[0]
    length = channel_major.shape[1]
    frequency = jnp.exp(pair_ids.astype(jnp.float32) * (-2.0 * math.log(rope_base) / HD))
    positions = jnp.arange(length, dtype=jnp.int32).astype(jnp.float32)
    angles = frequency[:, None] * positions[None, :]
    cos_table = jnp.cos(angles)
    sine_table = jnp.sin(angles)
    paired = channel_major.reshape(channels // 2, 2, length)
    even_part = paired[:, 0]
    odd_part = paired[:, 1]
    rotated = jnp.stack(
        [
            even_part * cos_table - odd_part * sine_table,
            even_part * sine_table + odd_part * cos_table,
        ],
        axis=1,
    )
    return rotated.reshape(channels, length)


def head_rows(table, kv_index):
    length = table.shape[1]
    grouped = table.reshape(HD // 2, KV_HEADS, 2, length)
    picked = lax.dynamic_slice_in_dim(grouped, kv_index, 1, 1)
    return picked.reshape(HD, length)


def normalize(hidden_in, gain_row):
    as_float = hidden_in.astype(jnp.float32)
    mean_square = jnp.mean(as_float * as_float, axis=1, keepdims=True)
    normed = (as_float * lax.rsqrt(mean_square + norm_eps) * gain_row).astype(jnp.bfloat16)
    return (as_float, normed)


def channel_product(weights, normed):
    return lax.dot_general(
        weights, normed, (((1,), (1,)), ((), ())), preferred_element_type=jnp.float32
    )


def local(arriving, norm_gain, w_query, w_key, w_value, w_out):
    local_block = arriving[0]
    gain_row = norm_gain[0].astype(jnp.float32)
    query_weights = w_query[0]
    key_weights = w_key[0]
    value_weights = w_value[0]
    out_weights = w_out[0]
    mp_count = lax.axis_size("mp")
    member = lax.axis_index("mp")
    length = local_block.shape[0]
    row_count = length // mp_count
    arrived = shifted(local_block, "section", 1)
    whole_rows = lax.all_gather(arrived, "mp", axis=1, tiled=True)
    full_float, normed_all = normalize(whole_rows, gain_row)
    residual = lax.dynamic_slice_in_dim(full_float, member * row_count, row_count, 0)
    projected = jnp.concatenate(
        [
            channel_product(query_weights, normed_all),
            channel_product(key_weights, normed_all),
            channel_product(value_weights, normed_all),
        ],
        axis=0,
    )
    q_width = query_weights.shape[0]
    k_width = key_weights.shape[0]
    query_pairs = jnp.arange(q_width // 2, dtype=jnp.int32) * 2 % HD // 2
    query_part = rotate_pairs(projected[:q_width], query_pairs).astype(jnp.bfloat16)
    key_pairs = (member * k_width + jnp.arange(k_width // 2, dtype=jnp.int32) * 2) // (2 * KV_HEADS)
    key_part = rotate_pairs(projected[q_width : q_width + k_width], key_pairs).astype(jnp.bfloat16)
    value_part = projected[q_width + k_width :].astype(jnp.bfloat16)
    key_all, value_all = (
        lax.all_gather(key_part, "mp", axis=0, tiled=True),
        lax.all_gather(value_part, "mp", axis=0, tiled=True),
    )
    local_heads = q_width // HD
    group_size = local_heads * mp_count // KV_HEADS
    kv_index = member * local_heads // group_size
    key_head = head_rows(key_all, kv_index)
    value_head = head_rows(value_all, kv_index)
    query_heads = query_part.reshape(local_heads, HD, length)
    score_scale = 1.0 / math.sqrt(HD)
    scores = (
        jnp.einsum("hdi,dj->hij", query_heads, key_head, preferred_element_type=jnp.float32)
        * score_scale
    )
    token_index = jnp.arange(length, dtype=jnp.int32)
    causal = token_index[:, None] >= token_index[None, :]
    scores = jnp.where(causal[None], scores, -1e30)
    row_max = jnp.max(scores, axis=-1, keepdims=True)
    exponent = jnp.exp(scores - row_max)
    row_total = jnp.sum(exponent, axis=-1, keepdims=True)
    weights = (exponent / row_total).astype(jnp.bfloat16)
    context = jnp.einsum(
        "hij,dj->ihd", weights, value_head, preferred_element_type=jnp.float32
    ).astype(jnp.bfloat16)
    context = context.reshape(length, q_width)
    full_term = jnp.dot(context, out_weights, preferred_element_type=jnp.float32)
    summed = lax.psum_scatter(
        full_term.astype(jnp.bfloat16), "mp", scatter_dimension=0, tiled=True
    ).astype(jnp.float32)
    attended = summed.astype(jnp.bfloat16)[None]
    stream_next = (residual + summed).astype(jnp.bfloat16)[None]
    return (attended, stream_next)


def solution(mesh):
    return jax.shard_map(
        local,
        mesh=mesh,
        in_specs=(
            P("section", None, "mp"),
            P("section", None),
            P("section", "mp", None),
            P("section", "mp", None),
            P("section", "mp", None),
            P("section", "mp", None),
        ),
        out_specs=(P("section", "mp", None), P("section", "mp", None)),
        check_vma=False,
    )
```

profile of v0, /device:TPU:4, one launch (start us, length us, event | category | flops | bytes accessed | tf_op | source)
XLA Modules:
  0.0 551.2 jit_solution(1898910907793692140)
XLA Ops:
  7.2 0.0 copy-start
  7.2 0.0 all-gather.4.cloned.1.call-start
  7.2 0.1 collective-permute-start
  7.3 20.1 %collective-permute-done = bf16[768,1024]{1,0:T(8,128)(2,1)} collective-permute-done((bf16[768,1024]{1,0:T(8,128)(2,1)}, bf16[768,1024]{1,0:T(8,128)(2,1)}, u32[]{:S(2)}, u32[]{:S(2)}) %collective-permute-start) | collective-permute-done | bytes 1572896 | tf_op jit(solution)/shard_map/ppermute | solution.py:19
  27.4 0.0 all-gather.4.cloned.1.call-update
  27.5 0.0 all-gather.6.cloned.1.call-start
  27.5 0.8 mul.223
  28.3 176.6 %all-gather.4.cloned.1.call-done = bf16[768,8192]{1,0:T(8,128)(2,1)} async-done(((bf16[768,1024]{1,0:T(8,128)(2,1)}), bf16[768,8192]{1,0:T(8,128)(2,1)}) %all-gather.4.cloned.1.call-update) | async-done | bytes 12582928 | tf_op jit(solution)/shard_map/all_gather | solution.py:75
  204.9 7.1 %multiply_reduce_fusion = f32[768]{0:T(1024)S(1)} fusion(bf16[768,8192]{1,0:T(8,128)(2,1)} %all-gather.4.cloned.1.call-done), kind=kLoop, calls=%fused_computation.2 | loop fusion | flops 18873600 | bytes 12585984 | tf_op jit(solution)/shard_map/reduce_sum | solution.py:52
  212.0 7.5 %multiply_convert_fusion = bf16[768,8192]{1,0:T(8,128)(2,1)S(1)} fusion(f32[8192]{0:T(1024)S(1)} %bitcast.56, f32[768]{0:T(1024)S(1)} %add_rsqrt_fusion, bf16[768,8192]{1,0:T(8,128)(2,1)} %all-gather.4.cloned.1.call-done), kind=kLoop, calls=%fused_computation.1 | loop fusion | flops 25165824 | bytes 25201664 | tf_op jit(solution)/shard_map/convert_element_type | solution.py:53
  219.5 0.0 copy-start.2
  219.5 4.5 copy-done.2
  224.0 0.0 copy-done
  224.0 4.1 fusion.24
  228.1 0.0 all-gather.6.cloned.1.call-update
  228.1 0.0 all-gather.8.cloned.1.call-start
  228.2 9.4 %fusion.18 = f32[128,768]{1,0:T(8,128)S(1)} fusion(bf16[768,8192]{1,0:T(8,128)(2,1)} %copy-done.2, bf16[1,128,8192]{2,1,0:T(8,128)(2,1)} %param.9), kind=kOutput, calls=%fused_computation.24 | convolution fusion | flops 1610612736 | bytes 15073280 | tf_op jit(solution)/shard_map/dot_general | solution.py:58
  237.7 0.2 reshape.284
  237.9 0.3 fusion.56
  238.2 0.8 fusion.42
  239.1 0.2 copy.22
  239.3 0.8 convert_element_type.92
  240.0 0.0 all-gather.8.cloned.1.call-update
  240.1 0.0 reduce-scatter.2.cloned.1.call-start
  240.2 0.2 iota_compare_fusion
  240.3 14.1 %fusion.14 = f32[256,768]{1,0:T(8,128)S(1)} fusion(bf16[768,8192]{1,0:T(8,128)(2,1)} %copy-done.2, bf16[1,256,8192]{2,1,0:T(8,128)(2,1)} %param.8), kind=kOutput, calls=%fused_computation.22 | convolution fusion | flops 3221225472 | bytes 17563648 | tf_op jit(solution)/shard_map/dot_general | solution.py:58
  254.4 0.5 reshape.283
  254.9 0.6 fusion.55
  255.5 1.7 fusion.34
  257.2 0.4 copy.19
  257.6 0.1 convert_element_type.90
  257.8 13.1 %all-gather.6.cloned.1.call-done = bf16[1024,768]{0,1:T(8,128)(2,1)} async-done(((bf16[128,768]{0,1:T(8,128)(2,1)}), bf16[1024,768]{0,1:T(8,128)(2,1)}) %all-gather.6.cloned.1.call-update) | async-done | bytes 1572880 | tf_op jit(solution)/shard_map/all_gather | solution.py:95
  270.9 1.7 copy.16
  272.6 1.5 reshape.281
  274.1 42.1 %all-gather.8.cloned.1.call-done = bf16[1024,768]{1,0:T(8,128)(2,1)} async-done(((bf16[128,768]{1,0:T(8,128)(2,1)}), bf16[1024,768]{1,0:T(8,128)(2,1)}) %all-gather.8.cloned.1.call-update) | async-done | bytes 1572880 | tf_op jit(solution)/shard_map/all_gather | solution.py:94
  316.2 3.5 reshape.285
  319.7 1.2 constant_dynamic-slice_fusion
  320.9 0.1 reshape.286
  321.0 0.1 reshape.290
  321.1 3.8 fusion.57
  324.9 0.0 copy-start.3
  324.9 3.0 fusion.17
  327.9 0.6 copy-done.3
  328.5 6.3 %convolution_convert_fusion = bf16[768,8192]{1,0:T(8,128)(2,1)} fusion(bf16[768,256]{0,1:T(8,128)(2,1)S(1)} %bitcast.55, bf16[1,256,8192]{2,1,0:T(8,128)(2,1)S(1)} %copy-done.3), kind=kOutput, calls=%fused_computation.3 | convolution fusion | flops 3227516928 | bytes 17170432 | tf_op jit(solution)/shard_map/dot_general | solution.py:119
  334.9 0.0 reduce-scatter.2.cloned.1.call-update
  334.9 0.0 copy-start.1
  334.9 14.5 %convert_element_type.84 = f32[768,8192]{1,0:T(8,128)} convert(bf16[768,8192]{1,0:T(8,128)(2,1)} %all-gather.4.cloned.1.call-done) | non-fusion elementwise | flops 6291456 | bytes 37748736 | tf_op jit(solution)/shard_map/convert_element_type | solution.py:51
  349.4 191.5 %reduce-scatter.2.cloned.1.call-done = bf16[96,8192]{1,0:T(8,128)(2,1)} async-done(((bf16[768,8192]{1,0:T(8,128)(2,1)}), bf16[96,8192]{1,0:T(8,128)(2,1)}) %reduce-scatter.2.cloned.1.call-update) | async-done | bytes 1572880 | tf_op jit(solution)/shard_map/reduce_scatter | solution.py:120
  540.8 3.8 fusion.13
  544.6 0.0 copy-done.1
  (6 shorter events, 0.1 us)
Async XLA Ops:
  7.2 216.9 %copy-start = (bf16[1,128,8192]{2,1,0:T(8,128)(2,1)S(1)}, bf16[1,128,8192]{2,1,0:T(8,128)(2,1)}, u32[]{:S(2)}) copy-start(bf16[1,128,8192]{2,1,0:T(8,128)(2,1)} %param.10) | copy-start | bytes 6291460
  7.2 197.7 %all-gather.4.cloned.1.call-start = ((), (), s32[]{:S(2)}) async-start(), calls=%async_computation.1 | async-start | bytes 14155776 | tf_op jit(solution)/shard_map/all_gather | solution.py:75
  7.2 20.2 %collective-permute-start = (bf16[768,1024]{1,0:T(8,128)(2,1)}, bf16[768,1024]{1,0:T(8,128)(2,1)}, u32[]{:S(2)}, u32[]{:S(2)}) collective-permute-start(bf16[768,1024]{1,0:T(8,128)(2,1)} %bitcast.57), channel_id=1, source_target_pairs={{24,0},{0,8},{8,16},{16,24},{25,1},{1,9},{9,17},{17,25},{26,2},{2,... | collective-permute-start | bytes 4718600 | tf_op jit(solution)/shard_map/ppermute | solution.py:19
  27.5 243.5 %all-gather.6.cloned.1.call-start = ((), (), s32[]{:S(2)}) async-start(), calls=%async_computation.2 | async-start | bytes 1769472 | tf_op jit(solution)/shard_map/all_gather | solution.py:95
  219.5 4.5 copy-start.2
  228.1 88.0 %all-gather.8.cloned.1.call-start = ((), (), s32[]{:S(2)}) async-start(), calls=%async_computation.3 | async-start | bytes 1769472 | tf_op jit(solution)/shard_map/all_gather | solution.py:94
  240.1 300.8 %reduce-scatter.2.cloned.1.call-start = ((), (), s32[]{:S(2)}) async-start(), calls=%async_computation.4 | async-start | bytes 14155776 | tf_op jit(solution)/shard_map/reduce_scatter | solution.py:120
  324.9 3.6 copy-start.3
  334.9 209.8 %copy-start.1 = (bf16[1,128,8192]{2,1,0:T(8,128)(2,1)S(1)}, bf16[1,128,8192]{2,1,0:T(8,128)(2,1)}, u32[]{:S(2)}) copy-start(bf16[1,128,8192]{2,1,0:T(8,128)(2,1)} %param.10) | copy-start | bytes 6291460
Sparse Core Ops, SparseCore 0:
  27.6 177.2 all-gather.3
  228.3 42.5 all-gather.5
  273.7 42.4 all-gather.7
  335.0 205.7 reduce-scatter.1
where the time goes:
time: 553 us; the launch traced here: 551 us
  waiting for transfers between devices  443 us (80%)
  matrix products  40.7 us (7%)
  other arithmetic  36.4 us (7%)
  local copies, waits for them, and re-layouts  16.4 us (3%)
  between operations  14 us (3%)
    reduce_scatter x1, waiting for transfers between devices, local(): lax.psum_scatter(full_term.astype(jnp.bfloat16), 'mp', scatter_dimension=...  191 us
    all_gather x1, waiting for transfers between devices, local(): whole_rows = lax.all_gather(arrived, 'mp', axis=1, tiled=True)  177 us
    all_gather x1, waiting for transfers between devices, local(): lax.all_gather(key_part, 'mp', axis=0, tiled=True)  42.1 us
    dot_general x3, matrix products, channel_product(): lax.dot_general(weights, normed, (((1,), (1,)), ((), ())), preferred_elem...  27.6 us
    ppermute x1, waiting for transfers between devices, shifted(): return lax.ppermute(block, axis, route)  20.1 us
    convert_element_type x1, other arithmetic, normalize(): as_float = hidden_in.astype(jnp.float32)  14.5 us
    all_gather x1, waiting for transfers between devices, local(): lax.all_gather(value_part, 'mp', axis=0, tiled=True)  13.1 us
  transfers between devices with their start and end apart: 5, of which 5 were waited for; matrix products, arithmetic and copies ran while one was open for 9% of the time, Pallas kernels for 0%

commit v1 on v0

v1 whole, which is shorter than its diff:
```python
import functools
import math

import jax
import jax.numpy as jnp
import numpy as np
from jax import lax
from jax.experimental import pallas as pl
from jax.experimental.pallas import tpu as pltpu
from jax.sharding import PartitionSpec as P

HD = 128
KV_HEADS = 8
ROPE_BASE = 500000.0
NORM_EPS = 1e-05
MESH = pl.DeviceIdType.MESH
VMEM_LIMIT = 64000000


def ring_position(member, n):
    return jnp.where(member % 2 == 0, member // 2, n - 1 - member // 2)


def ring_member(position, n):
    position = lax.rem(position + 2 * n, n)
    return jnp.where(position < n // 2, 2 * position, 2 * (n - 1 - position) + 1)


def swap_pairs(x):
    lane = lax.broadcasted_iota(jnp.int32, x.shape, 1)
    width = x.shape[1]
    return jnp.where(lane % 2 == 0, pltpu.roll(x, width - 1, 1), pltpu.roll(x, 1, 1))


def gather_kernel(
    n, chunks, arriving, gain, wq, wk, wv, cos_ref, sin_ref,
    q_out, k_out, v_out, resid_out,
    x_all, weights, acc, squares, w_sem, shift_send, shift_recv, ring_send, ring_recv,
):
    sections = lax.axis_size("section")
    section = lax.axis_index("section")
    me = lax.axis_index("mp")
    position = ring_position(me, n)
    right, left = ring_member(position + 1, n), ring_member(position - 1, n)
    following, previous = lax.rem(section + 1, sections), lax.rem(section + sections - 1, sections)
    hops = n // 2
    per = n // chunks
    rows = x_all.shape[2]
    width = x_all.shape[3]
    chunk_rows = per * rows
    qw, kw, vw = wq.shape[0], wk.shape[0], wv.shape[0]

    def weight_copy(j, part):
        src, start, size = ((wq, 0, qw), (wk, qw, kw), (wv, qw + kw, vw))[part]
        return pltpu.make_async_copy(
            src.at[:, pl.ds(j * width, width)], weights.at[j, pl.ds(start, size)], w_sem.at[j, part]
        )

    barrier = pltpu.get_barrier_semaphore()
    for partner in (right, left):
        pl.semaphore_signal(barrier, inc=1, device_id={"mp": partner}, device_id_type=MESH)
    for partner in (following, previous):
        pl.semaphore_signal(barrier, inc=1, device_id={"section": partner}, device_id_type=MESH)
    pl.semaphore_wait(barrier, 4)

    def shift_copy(c):
        return pltpu.make_async_remote_copy(
            src_ref=arriving.at[pl.ds(c * per, per)],
            dst_ref=x_all.at[me, pl.ds(c * per, per)],
            send_sem=shift_send.at[c], recv_sem=shift_recv.at[c],
            device_id={"section": following}, device_id_type=MESH,
        )

    def ring_copy(way, hop, c):
        origin = ring_member(position - (hop - 1) if way == 0 else position + (hop - 1), n)
        return pltpu.make_async_remote_copy(
            src_ref=x_all.at[origin, pl.ds(c * per, per)],
            dst_ref=x_all.at[origin, pl.ds(c * per, per)],
            send_sem=ring_send.at[way, hop - 1, c], recv_sem=ring_recv.at[way, hop - 1, c],
            device_id={"mp": right if way == 0 else left}, device_id_type=MESH,
        )

    for c in range(chunks):
        shift_copy(c).start()
    for j in range(n):
        for part in range(3):
            weight_copy(j, part).start()
    acc[...] = jnp.zeros_like(acc)
    squares[...] = jnp.zeros_like(squares)

    def compute(slot, c):
        x = x_all[slot, pl.ds(c * per, per)].astype(jnp.float32).reshape(chunk_rows, width)
        total = x[:, :128] * x[:, :128]
        for g in range(1, width // 128):
            part = x[:, g * 128 : (g + 1) * 128]
            total = total + part * part
        squares[c] += total
        scaled = (x * gain[slot]).astype(jnp.bfloat16)
        acc[c] += lax.dot_general(
            scaled, weights[slot], (((1,), (1,)), ((), ())), preferred_element_type=jnp.float32
        )

    for c in range(chunks):
        shift_copy(c).wait_recv()
        ring_copy(0, 1, c).start()
        ring_copy(1, 1, c).start()
    for j in range(n):
        for part in range(3):
            weight_copy(j, part).wait()

    @pl.loop(0, chunks)
    def _(c):
        compute(me, c)

    @pl.loop(0, hops * chunks)
    def _(i):
        hop = i // chunks + 1
        c = lax.rem(i, chunks)
        last = hop == hops
        low = c < chunks // 2
        for way in range(2):
            mine = low if way == 0 else jnp.logical_not(low)
            origin = ring_member(position - hop if way == 0 else position + hop, n)

            @pl.when(jnp.logical_or(jnp.logical_not(last), mine))
            def _():
                ring_copy(way, hop, c).wait_recv()

            @pl.when(jnp.logical_and(hop < hops, jnp.logical_or(hop + 1 < hops, mine)))
            def _():
                ring_copy(way, hop + 1, c).start()

        @pl.loop(0, 2)
        def _(way):
            mine = low == (way == 0)

            @pl.when(jnp.logical_or(jnp.logical_not(last), mine))
            def _():
                compute(ring_member(jnp.where(way == 0, position - hop, position + hop), n), c)

    inverse = lax.rsqrt(
        jnp.sum(squares[...].reshape(chunks * chunk_rows, 128), axis=1, keepdims=True) * (1.0 / (n * width)) + NORM_EPS
    )
    cos, sin = cos_ref[...], sin_ref[...]
    projected = acc[...].reshape(chunks * chunk_rows, qw + kw + vw) * inverse
    for h in range(qw // HD):
        q = projected[:, h * HD : (h + 1) * HD]
        q_out[:, h * HD : (h + 1) * HD] = (q * cos + swap_pairs(q) * sin).astype(jnp.bfloat16)

    lane = lax.broadcasted_iota(jnp.int32, (HD, kw), 1)
    source = lax.broadcasted_iota(jnp.int32, (HD, kw), 0)
    pick = (source == (me * kw + lane) // (2 * KV_HEADS) * 2 + lane % 2).astype(jnp.float32)
    nn = (((1,), (0,)), ((), ()))
    k_cos = lax.dot_general(cos, pick, nn, precision=lax.Precision.HIGHEST, preferred_element_type=jnp.float32)
    k_sin = lax.dot_general(sin, pick, nn, precision=lax.Precision.HIGHEST, preferred_element_type=jnp.float32)
    k = projected[:, qw : qw + kw]
    k_rot = (k * k_cos + swap_pairs(k) * k_sin).astype(jnp.bfloat16)
    v_bf = projected[:, qw + kw :].astype(jnp.bfloat16)
    per_head = kw // KV_HEADS
    target = lax.broadcasted_iota(jnp.int32, (kw, kw), 0)
    origin_row = lax.broadcasted_iota(jnp.int32, (kw, kw), 1)
    head, within = target // per_head, target % per_head
    order = (origin_row == (within // 2 * KV_HEADS + head) * 2 + within % 2).astype(jnp.bfloat16)
    nt = (((1,), (1,)), ((), ()))
    k_out[...] = lax.dot_general(order, k_rot, nt, preferred_element_type=jnp.float32).astype(jnp.bfloat16)
    v_out[...] = lax.dot_general(order, v_bf, nt, preferred_element_type=jnp.float32).astype(jnp.bfloat16)
    for j in range(n):
        resid_out[:, j * width : (j + 1) * width] = x_all[j, me]

    for c in range(chunks):
        shift_copy(c).wait_send()

    @pl.loop(0, hops * chunks)
    def _(i):
        hop = i // chunks + 1
        c = lax.rem(i, chunks)
        for way in range(2):
            mine = (c < chunks // 2) if way == 0 else (c >= chunks // 2)

            @pl.when(jnp.logical_or(hop < hops, mine))
            def _():
                ring_copy(way, hop, c).wait_send()


def scatter_kernel(
    n, pieces, q_ref, k_ref, v_ref, w_hbm, resid_ref,
    attended_ref, stream_ref,
    w_out, context, running, w_sem, send_sem, recv_sem,
):
    me = lax.axis_index("mp")
    position = ring_position(me, n)
    right, left = ring_member(position + 1, n), ring_member(position - 1, n)
    rows = q_ref.shape[1]
    length = n * rows
    heads = q_ref.shape[2] // HD
    width = running.shape[4]
    w_copy = pltpu.make_async_copy(w_hbm, w_out, w_sem)
    w_copy.start()

    barrier = pltpu.get_barrier_semaphore()
    for partner in (right, left):
        pl.semaphore_signal(barrier, inc=1, device_id={"mp": partner}, device_id_type=MESH)

    scale = 1.0 / math.sqrt(HD)

    def attend(block):
        row = lax.broadcasted_iota(jnp.int32, (rows, length), 0) + block * rows
        column = lax.broadcasted_iota(jnp.int32, (rows, length), 1)
        for h in range(heads):
            q = q_ref[block, :, h * HD : (h + 1) * HD]
            scores = lax.dot_general(
                q, k_ref[...], (((1,), (0,)), ((), ())), preferred_element_type=jnp.float32
            ) * scale
            scores = jnp.where(row >= column, scores, -1e30)
            exponent = jnp.exp(scores - jnp.max(scores, axis=1, keepdims=True))
            probs = (exponent / jnp.sum(exponent, axis=1, keepdims=True)).astype(jnp.bfloat16)
            context[block, :, h * HD : (h + 1) * HD] = lax.dot_general(
                probs, v_ref[...], (((1,), (1,)), ((), ())), preferred_element_type=jnp.float32
            ).astype(jnp.bfloat16)

    def block_of(way, step):
        return ring_member(position - 1 - step if way == 0 else position + 1 + step, n)

    def term(way, step, piece):
        start = (way * pieces + piece) * width
        return jnp.dot(
            context[block_of(way, step)], w_out[:, start : start + width], preferred_element_type=jnp.float32
        )

    def copy(way, step, piece):
        return pltpu.make_async_remote_copy(
            src_ref=running.at[way, step, piece],
            dst_ref=running.at[way, step + 1, piece],
            send_sem=send_sem.at[way, step, piece], recv_sem=recv_sem.at[way, step, piece],
            device_id={"mp": right if way == 0 else left}, device_id_type=MESH,
        )

    attend(block_of(0, 0))
    attend(block_of(1, 0))
    w_copy.wait()
    pl.semaphore_wait(barrier, 2)
    for piece in range(pieces):
        for way in range(2):
            running[way, 0, piece] = term(way, 0, piece).astype(jnp.bfloat16)
            copy(way, 0, piece).start()

    def ahead(step):
        @pl.when(step < n // 2)
        def _():
            attend(block_of(0, step))
            attend(block_of(1, step))

        @pl.when(step == n // 2)
        def _():
            attend(me)

    ahead(1)

    @pl.loop(1, n - 1)
    def _(step):
        for piece in range(pieces):
            for way in range(2):
                value = term(way, step, piece)
                copy(way, step - 1, piece).wait_recv()
                running[way, step, piece] = (running[way, step, piece].astype(jnp.float32) + value).astype(jnp.bfloat16)
                copy(way, step, piece).start()
        ahead(step + 1)

    for piece in range(pieces):
        for way in range(2):
            value = term(way, n - 1, piece)
            copy(way, n - 2, piece).wait_recv()
            value = running[way, n - 1, piece].astype(jnp.float32) + value
            columns = slice((way * pieces + piece) * width, (way * pieces + piece + 1) * width)
            attended_ref[:, columns] = value.astype(jnp.bfloat16)
            stream_ref[:, columns] = (resid_ref[:, columns].astype(jnp.float32) + value).astype(jnp.bfloat16)

    @pl.loop(0, n - 1)
    def _(step):
        for piece in range(pieces):
            for way in range(2):
                copy(way, step, piece).wait_send()


def rotary_tables(length):
    pair = (np.arange(HD) // 2).astype(np.float32)
    frequency = np.exp(pair * np.float32(-2.0 * math.log(ROPE_BASE) / HD)).astype(np.float32)
    angles = frequency[None, :] * np.arange(length, dtype=np.float32)[:, None]
    sign = np.where(np.arange(HD) % 2 == 0, -1.0, 1.0).astype(np.float32)
    return np.cos(angles).astype(np.float32), (np.sin(angles) * sign).astype(np.float32)


def local(arriving, norm_gain, w_query, w_key, w_value, w_out):
    n = lax.axis_size("mp")
    length, width = arriving.shape[1:]
    rows = length // n
    full = n * width
    chunks = 4 if n <= 8 else 2
    pieces = 4 if n <= 8 else 2
    qw, kw, vw = w_query.shape[1], w_key.shape[1], w_value.shape[1]
    cos, sin = rotary_tables(length)
    vmem = pl.BlockSpec(memory_space=pltpu.VMEM)
    anywhere = pl.BlockSpec(memory_space=pl.ANY)
    bf16, f32 = jnp.bfloat16, jnp.float32
    dma = pltpu.SemaphoreType.DMA
    q, k, v, resid = pl.pallas_call(
        functools.partial(gather_kernel, n, chunks),
        name="gather_project",
        out_shape=(
            jax.ShapeDtypeStruct((length, qw), bf16),
            jax.ShapeDtypeStruct((kw, length), bf16),
            jax.ShapeDtypeStruct((vw, length), bf16),
            jax.ShapeDtypeStruct((rows, full), bf16),
        ),
        in_specs=[anywhere, vmem, anywhere, anywhere, anywhere, vmem, vmem],
        out_specs=(vmem,) * 4,
        scratch_shapes=[
            pltpu.VMEM((n, n, rows, width), bf16),
            pltpu.VMEM((n, qw + kw + vw, width), bf16),
            pltpu.VMEM((chunks, length // chunks, qw + kw + vw), f32),
            pltpu.VMEM((chunks, length // chunks, 128), f32),
            dma((n, 3)),
            dma((chunks,)),
            dma((chunks,)),
            dma((2, n // 2, chunks)),
            dma((2, n // 2, chunks)),
        ],
        compiler_params=pltpu.CompilerParams(collective_id=0, has_side_effects=True, vmem_limit_bytes=VMEM_LIMIT),
    )(
        arriving[0].reshape(n, rows, width),
        norm_gain[0].astype(f32).reshape(n, 1, width),
        w_query[0], w_key[0], w_value[0], jnp.asarray(cos), jnp.asarray(sin),
    )
    per_head = kw // KV_HEADS
    sent = jnp.stack([k.reshape(KV_HEADS, per_head, length), v.reshape(KV_HEADS, per_head, length)], axis=1)
    local_heads = qw // HD
    group_size = local_heads * n // KV_HEADS
    if n != KV_HEADS:
        sent = sent[np.arange(n) * local_heads // group_size]
    got = lax.all_to_all(sent, "mp", 0, 0, tiled=True)
    key_head = got[:, 0].reshape(HD, length)
    value_head = got[:, 1].reshape(HD, length)
    attended, stream = pl.pallas_call(
        functools.partial(scatter_kernel, n, pieces),
        name="attend_scatter",
        out_shape=(jax.ShapeDtypeStruct((rows, full), bf16),) * 2,
        in_specs=[vmem, vmem, vmem, anywhere, vmem],
        out_specs=(vmem, vmem),
        scratch_shapes=[
            pltpu.VMEM((qw, full), bf16),
            pltpu.VMEM((n, rows, qw), bf16),
            pltpu.VMEM((2, n, pieces, rows, full // (2 * pieces)), bf16),
            dma(()),
            dma((2, n - 1, pieces)),
            dma((2, n - 1, pieces)),
        ],
        compiler_params=pltpu.CompilerParams(collective_id=1, has_side_effects=True, vmem_limit_bytes=VMEM_LIMIT),
    )(q.reshape(n, rows, qw), key_head, value_head, w_out[0], resid)
    return (attended[None], stream[None])


def solution(mesh):
    return jax.shard_map(
        local,
        mesh=mesh,
        in_specs=(
            P("section", None, "mp"),
            P("section", None),
            P("section", "mp", None),
            P("section", "mp", None),
            P("section", "mp", None),
            P("section", "mp", None),
        ),
        out_specs=(P("section", "mp", None), P("section", "mp", None)),
        check_vma=False,
    )
```

time: 553 us -> 274 us (0.50)
  waiting for transfers between devices: 443 us -> 0 us
  Pallas kernels: 0 us -> 251 us
  matrix products: 40.7 us -> 0 us
  other arithmetic: 36.4 us -> 2.47 us
  blocking collectives: 0 us -> 14 us
  between operations: 14 us -> 0.66 us
  local copies, waits for them, and re-layouts: 16.4 us -> 4.68 us
    pallas_call x0 -> x2, Pallas kernels: none -> 251 us  [the longest x1 130 us: local(): pl.pallas_call(functools.partial(gather_kernel, n, chunks), name='gather_...]
    all_gather x3 -> x0, waiting for transfers between devices: 232 us -> none  [the longest x1 177 us: local(): whole_rows = lax.all_gather(arrived, 'mp', axis=1, tiled=True)]
    reduce_scatter x1 -> x0, waiting for transfers between devices: 191 us -> none  [local(): lax.psum_scatter(full_term.astype(jnp.bfloat16), 'mp', scatter_dimension=...]
    dot_general x5 -> x0, matrix products: 36.9 us -> none  [the longest x3 27.6 us: channel_product(): lax.dot_general(weights, normed, (((1,), (1,)), ((), ())), preferred_elem...]
    convert_element_type x3 -> x1, other arithmetic: 21.9 us -> 1.41 us  [local(): norm_gain[0].astype(f32).reshape(n, 1, width)]
    ppermute x1 -> x0, waiting for transfers between devices: 20.1 us -> none  [shifted(): return lax.ppermute(block, axis, route)]
    all_to_all x0 -> x1, blocking collectives: none -> 14 us  [local(): got = lax.all_to_all(sent, 'mp', 0, 0, tiled=True)]
    reduce_sum x1 -> x0, other arithmetic: 7.09 us -> none  [normalize(): mean_square = jnp.mean(as_float * as_float, axis=1, keepdims=True)]
  transfers between devices with their start and end apart: 5 -> 0, of which waited for: 5 -> 0; matrix products, arithmetic and copies ran while one was open for 9% -> 0% of each run, Pallas kernels for 0% -> 0%
where the time goes in v1:
time: 274 us; the launch traced here: 273 us
  Pallas kernels  251 us (92%)
  blocking collectives  14 us (5%)
  local copies, waits for them, and re-layouts  4.68 us (2%)
    pallas_call x1, Pallas kernels, local(): pl.pallas_call(functools.partial(gather_kernel, n, chunks), name='gather_...  130 us
    pallas_call x1, Pallas kernels, local(): pl.pallas_call(functools.partial(scatter_kernel, n, pieces), name='attend...  121 us
    all_to_all x1, blocking collectives, local(): got = lax.all_to_all(sent, 'mp', 0, 0, tiled=True)  14 us

profile of v1, /device:TPU:4, one launch (start us, length us, event | category | flops | bytes accessed | tf_op | source)
XLA Modules:
  0.0 273.1 jit_solution(16851270922445933936)
XLA Ops:
  0.6 1.4 convert.1.gain
  2.0 130.3 %gather_project.1 = (bf16[768,256]{1,0:T(8,128)(2,1)}, bf16[128,768]{1,0:T(8,128)(2,1)}, bf16[128,768]{1,0:T(8,128)(2,1)}, bf16[96,8192]{1,0:T(8,128)(2,1)}) custom-call(bf16[8,96,1024]{2,1,0:T(8,128)(2,1)} %bitcast.24, f32[8,1,1024]{2,1,0:T(1,128)} %convert.1.gain, bf16[256,8192]{1,0:T(8,128)(2,1)} %bitcast.19, bf16[128,8192]{1,0:T(8,128)(2,1)} %bitcast.20, ...), custom_call_target="tpu_custom_call" | custom-call | tf_op jit(solution)/shard_map/gather_project/pallas_call | solution.py:306
  132.3 1.1 pad_maximum_fusion
  133.4 14.0 %all_to_all.5 = bf16[8,2,16,768]{3,2,1,0:T(8,128)(2,1)S(1)} all-to-all(bf16[8,2,16,768]{3,2,1,0:T(8,128)(2,1)S(1)} %pad_maximum_fusion), channel_id=1, replica_groups=mesh['section'=4,'mp'=8] {'mp'}, dimensions={0} | all-to-all | bytes 786432 | tf_op jit(solution)/shard_map/all_to_all | solution.py:340
  147.4 0.8 fusion
  148.2 121.0 %attend_scatter.1 = (bf16[96,8192]{1,0:T(8,128)(2,1)}, bf16[96,8192]{1,0:T(8,128)(2,1)}) custom-call(bf16[8,96,256]{2,1,0:T(8,128)(2,1)} %bitcast.27, bf16[128,768]{1,0:T(8,128)(2,1)} %bitcast.26, bf16[128,768]{1,0:T(8,128)(2,1)} %bitcast.25, bf16[256,8192]{1,0:T(8,128)(2,1)} %bitcast.18, bf16[96,8192]{1,0:T(8,128)(2,1)} %get-tuple-element.11.resid_ref), custom_call_target="tpu_custom_call" | custom-call | tf_op jit(solution)/shard_map/attend_scatter/pallas_call | solution.py:343
  269.2 0.0 copy-start
  269.2 2.8 %copy.14 = bf16[1,96,8192]{2,1,0:T(8,128)(2,1)} copy(bf16[1,96,8192]{2,1,0:T(8,128)(2,1)} %bitcast.23) | data formatting | bytes 3145728
  272.0 0.0 copy-done
  272.0 1.1 copy.15
Async XLA Ops:
  269.2 2.8 %copy-start = (bf16[96,8192]{1,0:T(8,128)(2,1)S(1)}, bf16[96,8192]{1,0:T(8,128)(2,1)}, u32[]{:S(2)}) copy-start(bf16[96,8192]{1,0:T(8,128)(2,1)} %get-tuple-element.13) | copy-start | bytes 4718596

commit v2 on v1

v2 whole, which is shorter than its diff:
```python
import functools
import math

import jax
import jax.numpy as jnp
import numpy as np
from jax import lax
from jax.experimental import pallas as pl
from jax.experimental.pallas import tpu as pltpu
from jax.sharding import PartitionSpec as P

HD = 128
KV_HEADS = 8
ROPE_BASE = 500000.0
NORM_EPS = 1e-05
MESH = pl.DeviceIdType.MESH
VMEM_LIMIT = 64000000


def ring_position(member, n):
    return jnp.where(member % 2 == 0, member // 2, n - 1 - member // 2)


def ring_member(position, n):
    position = lax.rem(position + 2 * n, n)
    return jnp.where(position < n // 2, 2 * position, 2 * (n - 1 - position) + 1)


def swap_pairs(x):
    lane = lax.broadcasted_iota(jnp.int32, x.shape, 1)
    width = x.shape[1]
    return jnp.where(lane % 2 == 0, pltpu.roll(x, width - 1, 1), pltpu.roll(x, 1, 1))


def layer_kernel(
    n, chunks, pieces, arriving, gain, wq, wk, wv, w_hbm, cos_ref, sin_ref,
    attended_ref, stream_ref,
    x_all, weights, acc, squares, sent, got, heads_kv, key_head, value_head, q_ref, w_out, context, running,
    w_sem, wo_sem, shift_send, shift_recv, ring_send, ring_recv, kv_send, kv_recv, send_sem, recv_sem,
):
    sections = lax.axis_size("section")
    section = lax.axis_index("section")
    me = lax.axis_index("mp")
    position = ring_position(me, n)
    right, left = ring_member(position + 1, n), ring_member(position - 1, n)
    following, previous = lax.rem(section + 1, sections), lax.rem(section + sections - 1, sections)
    hops = n // 2
    per = n // chunks
    rows, width = x_all.shape[2:]
    length = n * rows
    chunk_rows = per * rows
    qw, kw, vw = wq.shape[0], wk.shape[0], wv.shape[0]
    heads = qw // HD
    group_size = heads * n // KV_HEADS
    nn = (((1,), (0,)), ((), ()))
    nt = (((1,), (1,)), ((), ()))

    barrier = pltpu.get_barrier_semaphore()
    for step in range(1, n):
        pl.semaphore_signal(barrier, inc=1, device_id={"mp": lax.rem(me + step, n)}, device_id_type=MESH)
    for partner in (following, previous):
        pl.semaphore_signal(barrier, inc=1, device_id={"section": partner}, device_id_type=MESH)

    def weight_copy(j, part):
        src, start, size = ((wq, 0, qw), (wk, qw, kw), (wv, qw + kw, vw))[part]
        return pltpu.make_async_copy(
            src.at[:, pl.ds(j * width, width)], weights.at[j, pl.ds(start, size)], w_sem.at[j, part]
        )

    def shift_copy(c):
        return pltpu.make_async_remote_copy(
            src_ref=arriving.at[pl.ds(c * per, per)],
            dst_ref=x_all.at[me, pl.ds(c * per, per)],
            send_sem=shift_send.at[c], recv_sem=shift_recv.at[c],
            device_id={"section": following}, device_id_type=MESH,
        )

    def ring_copy(way, hop, c):
        origin = ring_member(position - (hop - 1) if way == 0 else position + (hop - 1), n)
        return pltpu.make_async_remote_copy(
            src_ref=x_all.at[origin, pl.ds(c * per, per)],
            dst_ref=x_all.at[origin, pl.ds(c * per, per)],
            send_sem=ring_send.at[way, hop - 1, c], recv_sem=ring_recv.at[way, hop - 1, c],
            device_id={"mp": right if way == 0 else left}, device_id_type=MESH,
        )

    pl.semaphore_wait(barrier, n + 1)
    for c in range(chunks):
        shift_copy(c).start()
    for j in range(n):
        for part in range(3):
            weight_copy(j, part).start()
    acc[...] = jnp.zeros_like(acc)
    squares[...] = jnp.zeros_like(squares)

    def compute(slot, c):
        x = x_all[slot, pl.ds(c * per, per)].astype(jnp.float32).reshape(chunk_rows, width)
        total = x[:, :128] * x[:, :128]
        for g in range(1, width // 128):
            part = x[:, g * 128 : (g + 1) * 128]
            total = total + part * part
        squares[c] += total
        scaled = (x * gain[slot].astype(jnp.float32)).astype(jnp.bfloat16)
        acc[c] += lax.dot_general(scaled, weights[slot], nt, preferred_element_type=jnp.float32)

    for c in range(chunks):
        shift_copy(c).wait_recv()
        ring_copy(0, 1, c).start()
        ring_copy(1, 1, c).start()
    for j in range(n):
        for part in range(3):
            weight_copy(j, part).wait()
    wo_copy = pltpu.make_async_copy(w_hbm, w_out, wo_sem)
    wo_copy.start()

    @pl.loop(0, chunks)
    def _(c):
        compute(me, c)

    cos, sin = cos_ref[...], sin_ref[...]
    lane = lax.broadcasted_iota(jnp.int32, (HD, kw), 1)
    source = lax.broadcasted_iota(jnp.int32, (HD, kw), 0)
    pick = (source == (me * kw + lane) // (2 * KV_HEADS) * 2 + lane % 2).astype(jnp.float32)
    k_cos = lax.dot_general(cos, pick, nn, precision=lax.Precision.HIGHEST, preferred_element_type=jnp.float32)
    k_sin = lax.dot_general(sin, pick, nn, precision=lax.Precision.HIGHEST, preferred_element_type=jnp.float32)
    per_head = kw // KV_HEADS
    target = lax.broadcasted_iota(jnp.int32, (kw, kw), 0)
    origin_row = lax.broadcasted_iota(jnp.int32, (kw, kw), 1)
    head, within = target // per_head, target % per_head
    order = (origin_row == (within // 2 * KV_HEADS + head) * 2 + within % 2).astype(jnp.bfloat16)

    @pl.loop(0, hops * chunks)
    def _(i):
        hop = i // chunks + 1
        c = lax.rem(i, chunks)
        last = hop == hops
        low = c < chunks // 2
        for way in range(2):
            mine = low if way == 0 else jnp.logical_not(low)

            @pl.when(jnp.logical_or(jnp.logical_not(last), mine))
            def _():
                ring_copy(way, hop, c).wait_recv()

            @pl.when(jnp.logical_and(hop < hops, jnp.logical_or(hop + 1 < hops, mine)))
            def _():
                ring_copy(way, hop + 1, c).start()

        @pl.loop(0, 2)
        def _(way):
            mine = low == (way == 0)

            @pl.when(jnp.logical_or(jnp.logical_not(last), mine))
            def _():
                compute(ring_member(jnp.where(way == 0, position - hop, position + hop), n), c)

    inverse = lax.rsqrt(
        jnp.sum(squares[...].reshape(length, 128), axis=1, keepdims=True) * (1.0 / (n * width)) + NORM_EPS
    )
    k = acc[:, :, qw : qw + kw].reshape(length, kw) * inverse
    k_rot = (k * k_cos + swap_pairs(k) * k_sin).astype(jnp.bfloat16)
    v_bf = (acc[:, :, qw + kw :].reshape(length, vw) * inverse).astype(jnp.bfloat16)
    for part, rotated in enumerate((k_rot, v_bf)):
        ordered = lax.dot_general(order, rotated, nt, preferred_element_type=jnp.float32)
        for h in range(KV_HEADS):
            sent[h, part] = ordered[h * per_head : (h + 1) * per_head].astype(jnp.bfloat16)

    def kv_copy(step):
        other = lax.rem(me + step, n)
        return pltpu.make_async_remote_copy(
            src_ref=sent.at[other * heads // group_size], dst_ref=got.at[me],
            send_sem=kv_send.at[step - 1], recv_sem=kv_recv.at[step - 1],
            device_id={"mp": other}, device_id_type=MESH,
        )

    for step in range(1, n):
        kv_copy(step).start()
    got[me] = sent[me * heads // group_size]
    for h in range(heads):
        q = acc[:, :, h * HD : (h + 1) * HD].reshape(length, HD) * inverse
        q_ref[:, :, h * HD : (h + 1) * HD] = (
            (q * cos + swap_pairs(q) * sin).reshape(n, rows, HD).astype(jnp.bfloat16)
        )
    for step in range(1, n):
        kv_copy(step).wait_recv()
    for j in range(n):
        for part in range(2):
            heads_kv[part, j * per_head : (j + 1) * per_head] = got[j, part].astype(jnp.float32)
    key_head[...] = heads_kv[0].astype(jnp.bfloat16)
    value_head[...] = heads_kv[1].astype(jnp.bfloat16)

    piece_width = running.shape[4]
    scale = 1.0 / math.sqrt(HD)

    def attend(block):
        row = lax.broadcasted_iota(jnp.int32, (rows, length), 0) + block * rows
        column = lax.broadcasted_iota(jnp.int32, (rows, length), 1)
        for h in range(heads):
            q = q_ref[block, :, h * HD : (h + 1) * HD]
            scores = lax.dot_general(q, key_head[...], nn, preferred_element_type=jnp.float32) * scale
            scores = jnp.where(row >= column, scores, -1e30)
            exponent = jnp.exp(scores - jnp.max(scores, axis=1, keepdims=True))
            probs = (exponent / jnp.sum(exponent, axis=1, keepdims=True)).astype(jnp.bfloat16)
            context[block, :, h * HD : (h + 1) * HD] = lax.dot_general(
                probs, value_head[...], nt, preferred_element_type=jnp.float32
            ).astype(jnp.bfloat16)

    def block_of(way, step):
        return ring_member(position - 1 - step if way == 0 else position + 1 + step, n)

    def term(way, step, piece):
        start = (way * pieces + piece) * piece_width
        return jnp.dot(
            context[block_of(way, step)], w_out[:, start : start + piece_width], preferred_element_type=jnp.float32
        )

    def sum_copy(way, step, piece):
        return pltpu.make_async_remote_copy(
            src_ref=running.at[way, step, piece],
            dst_ref=running.at[way, step + 1, piece],
            send_sem=send_sem.at[way, step, piece], recv_sem=recv_sem.at[way, step, piece],
            device_id={"mp": right if way == 0 else left}, device_id_type=MESH,
        )

    wo_copy.wait()
    for way in range(2):
        attend(block_of(way, 0))
        for piece in range(pieces):
            running[way, 0, piece] = term(way, 0, piece).astype(jnp.bfloat16)
            sum_copy(way, 0, piece).start()

    def ahead(step):
        @pl.when(step < n // 2)
        def _():
            attend(block_of(0, step))
            attend(block_of(1, step))

        @pl.when(step == n // 2)
        def _():
            attend(me)

    ahead(1)

    @pl.loop(1, n - 1)
    def _(step):
        for piece in range(pieces):
            for way in range(2):
                value = term(way, step, piece)
                sum_copy(way, step - 1, piece).wait_recv()
                running[way, step, piece] = (running[way, step, piece].astype(jnp.float32) + value).astype(jnp.bfloat16)
                sum_copy(way, step, piece).start()
        ahead(step + 1)

    for j in range(n):
        stream_ref[:, j * width : (j + 1) * width] = x_all[j, me]
    for piece in range(pieces):
        for way in range(2):
            value = term(way, n - 1, piece)
            sum_copy(way, n - 2, piece).wait_recv()
            value = running[way, n - 1, piece].astype(jnp.float32) + value
            columns = slice((way * pieces + piece) * piece_width, (way * pieces + piece + 1) * piece_width)
            attended_ref[:, columns] = value.astype(jnp.bfloat16)
            stream_ref[:, columns] = (stream_ref[:, columns].astype(jnp.float32) + value).astype(jnp.bfloat16)

    for c in range(chunks):
        shift_copy(c).wait_send()
    for step in range(1, n):
        kv_copy(step).wait_send()

    @pl.loop(0, hops * chunks)
    def _(i):
        hop = i // chunks + 1
        c = lax.rem(i, chunks)
        for way in range(2):
            mine = (c < chunks // 2) if way == 0 else (c >= chunks // 2)

            @pl.when(jnp.logical_or(hop < hops, mine))
            def _():
                ring_copy(way, hop, c).wait_send()

    @pl.loop(0, n - 1)
    def _(step):
        for piece in range(pieces):
            for way in range(2):
                sum_copy(way, step, piece).wait_send()


def rotary_tables(length):
    pair = (np.arange(HD) // 2).astype(np.float32)
    frequency = np.exp(pair * np.float32(-2.0 * math.log(ROPE_BASE) / HD)).astype(np.float32)
    angles = frequency[None, :] * np.arange(length, dtype=np.float32)[:, None]
    sign = np.where(np.arange(HD) % 2 == 0, -1.0, 1.0).astype(np.float32)
    return np.cos(angles).astype(np.float32), (np.sin(angles) * sign).astype(np.float32)


def local(arriving, norm_gain, w_query, w_key, w_value, w_out):
    n = lax.axis_size("mp")
    length, width = arriving.shape[1:]
    rows = length // n
    full = n * width
    chunks = 8 if n <= 8 else 2
    pieces = 4 if n <= 8 else 2
    qw, kw, vw = w_query.shape[1], w_key.shape[1], w_value.shape[1]
    cos, sin = rotary_tables(length)
    vmem = pl.BlockSpec(memory_space=pltpu.VMEM)
    anywhere = pl.BlockSpec(memory_space=pl.ANY)
    bf16, f32 = jnp.bfloat16, jnp.float32
    dma = pltpu.SemaphoreType.DMA
    attended, stream = pl.pallas_call(
        functools.partial(layer_kernel, n, chunks, pieces),
        name="layer",
        out_shape=(jax.ShapeDtypeStruct((rows, full), bf16),) * 2,
        in_specs=[anywhere, vmem, anywhere, anywhere, anywhere, anywhere, vmem, vmem],
        out_specs=(vmem, vmem),
        scratch_shapes=[
            pltpu.VMEM((n, n, rows, width), bf16),
            pltpu.VMEM((n, qw + kw + vw, width), bf16),
            pltpu.VMEM((chunks, length // chunks, qw + kw + vw), f32),
            pltpu.VMEM((chunks, length // chunks, 128), f32),
            pltpu.VMEM((KV_HEADS, 2, kw // KV_HEADS, length), bf16),
            pltpu.VMEM((n, 2, kw // KV_HEADS, length), bf16),
            pltpu.VMEM((2, HD, length), f32),
            pltpu.VMEM((HD, length), bf16),
            pltpu.VMEM((HD, length), bf16),
            pltpu.VMEM((n, rows, qw), bf16),
            pltpu.VMEM((qw, full), bf16),
            pltpu.VMEM((n, rows, qw), bf16),
            pltpu.VMEM((2, n, pieces, rows, full // (2 * pieces)), bf16),
            dma((n, 3)),
            dma(()),
            dma((chunks,)),
            dma((chunks,)),
            dma((2, n // 2, chunks)),
            dma((2, n // 2, chunks)),
            dma((n - 1,)),
            dma((n - 1,)),
            dma((2, n - 1, pieces)),
            dma((2, n - 1, pieces)),
        ],
        compiler_params=pltpu.CompilerParams(collective_id=0, has_side_effects=True, vmem_limit_bytes=VMEM_LIMIT),
    )(
        arriving[0].reshape(n, rows, width),
        norm_gain[0].reshape(n, 1, width),
        w_query[0], w_key[0], w_value[0], w_out[0], jnp.asarray(cos), jnp.asarray(sin),
    )
    return (attended[None], stream[None])


def solution(mesh):
    return jax.shard_map(
        local,
        mesh=mesh,
        in_specs=(
            P("section", None, "mp"),
            P("section", None),
            P("section", "mp", None),
            P("section", "mp", None),
            P("section", "mp", None),
            P("section", "mp", None),
        ),
        out_specs=(P("section", "mp", None), P("section", "mp", None)),
        check_vma=False,
    )
```

time: 274 us -> 268 us (0.978)
  blocking collectives: 14 us -> 0 us
  Pallas kernels: 251 us -> 263 us
    all_to_all x1 -> x0, blocking collectives: 14 us -> none  [local(): got = lax.all_to_all(sent, 'mp', 0, 0, tiled=True)]
    pallas_call x2 -> x1, Pallas kernels: 251 us -> 263 us  [local(): pl.pallas_call(functools.partial(layer_kernel, n, chunks, pieces), name='...]
where the time goes in v2:
time: 268 us
  Pallas kernels  263 us (98%)
  local copies, waits for them, and re-layouts  3.92 us (1%)
    pallas_call x1, Pallas kernels, local(): pl.pallas_call(functools.partial(layer_kernel, n, chunks, pieces), name='...  263 us

profile of v2, /device:TPU:4, one launch (start us, length us, event | category | flops | bytes accessed | tf_op | source)
XLA Modules:
  0.0 267.9 jit_solution(15662525011288449014)
XLA Ops:
  0.6 263.3 %layer.1 = (bf16[96,8192]{1,0:T(8,128)(2,1)}, bf16[96,8192]{1,0:T(8,128)(2,1)}) custom-call(bf16[8,96,1024]{2,1,0:T(8,128)(2,1)} %bitcast.12, bf16[8,1,1024]{2,1,0:T(2,128)(2,1)} %bitcast.15, bf16[256,8192]{1,0:T(8,128)(2,1)} %bitcast.8, bf16[128,8192]{1,0:T(8,128)(2,1)} %bitcast.10, bf16[128,8192]{1,0:T(8,128)(2,1)} %bitcast.11, bf16[256,8192]{1,0:T(8,128)(2,1)} %bitcast.9, ...), custom_call_target="tpu_custom_call" | custom-call | tf_op jit(solution)/shard_map/layer/pallas_call | solution.py:309
  264.0 0.0 copy-start
  264.0 2.8 %copy.12 = bf16[1,96,8192]{2,1,0:T(8,128)(2,1)} copy(bf16[1,96,8192]{2,1,0:T(8,128)(2,1)} %bitcast.14) | data formatting | bytes 3145728
  266.8 0.0 copy-done
  266.8 1.1 copy.13
Async XLA Ops:
  264.0 2.8 %copy-start = (bf16[96,8192]{1,0:T(8,128)(2,1)S(1)}, bf16[96,8192]{1,0:T(8,128)(2,1)}, u32[]{:S(2)}) copy-start(bf16[96,8192]{1,0:T(8,128)(2,1)} %get-tuple-element.5) | copy-start | bytes 4718596

commit v3 on v2

--- a/solution.py
+++ b/solution.py
@@ -14,7 +14,7 @@
 ROPE_BASE = 500000.0
 NORM_EPS = 1e-05
 MESH = pl.DeviceIdType.MESH
-VMEM_LIMIT = 64000000
+VMEM_LIMIT = 52000000
 
 
 def ring_position(member, n):
@@ -33,10 +33,10 @@
 
 
 def layer_kernel(
-    n, chunks, pieces, arriving, gain, wq, wk, wv, w_hbm, cos_ref, sin_ref,
+    n, chunks, pieces, arriving, gain_hbm, wq, wk, wv, w_hbm, tables_hbm,
     attended_ref, stream_ref,
-    x_all, weights, acc, squares, sent, got, heads_kv, key_head, value_head, q_ref, w_out, context, running,
-    w_sem, wo_sem, shift_send, shift_recv, ring_send, ring_recv, kv_send, kv_recv, send_sem, recv_sem,
+    staged, gain, tables, x_all, weights, acc, squares, sent, got, heads_kv, key_head, value_head, q_ref, w_out, context, running,
+    stage_sem, gain_sem, tables_sem, w_sem, wo_sem, shift_send, shift_recv, ring_send, ring_recv, kv_send, kv_recv, send_sem, recv_sem,
 ):
     sections = lax.axis_size("section")
     section = lax.axis_index("section")
@@ -55,6 +55,12 @@
     nn = (((1,), (0,)), ((), ()))
     nt = (((1,), (1,)), ((), ()))
 
+    stage = pltpu.make_async_copy(arriving, staged, stage_sem)
+    stage.start()
+    gain_copy = pltpu.make_async_copy(gain_hbm, gain, gain_sem)
+    gain_copy.start()
+    tables_copy = pltpu.make_async_copy(tables_hbm, tables, tables_sem)
+    tables_copy.start()
     barrier = pltpu.get_barrier_semaphore()
     for step in range(1, n):
         pl.semaphore_signal(barrier, inc=1, device_id={"mp": lax.rem(me + step, n)}, device_id_type=MESH)
@@ -69,7 +75,7 @@
 
     def shift_copy(c):
         return pltpu.make_async_remote_copy(
-            src_ref=arriving.at[pl.ds(c * per, per)],
+            src_ref=staged.at[pl.ds(c * per, per)],
             dst_ref=x_all.at[me, pl.ds(c * per, per)],
             send_sem=shift_send.at[c], recv_sem=shift_recv.at[c],
             device_id={"section": following}, device_id_type=MESH,
@@ -84,12 +90,13 @@
             device_id={"mp": right if way == 0 else left}, device_id_type=MESH,
         )
 
+    for j in range(n):
+        for part in range(3):
+            weight_copy(j, part).start()
+    stage.wait()
     pl.semaphore_wait(barrier, n + 1)
     for c in range(chunks):
         shift_copy(c).start()
-    for j in range(n):
-        for part in range(3):
-            weight_copy(j, part).start()
     acc[...] = jnp.zeros_like(acc)
     squares[...] = jnp.zeros_like(squares)
 
@@ -110,6 +117,8 @@
     for j in range(n):
         for part in range(3):
             weight_copy(j, part).wait()
+    gain_copy.wait()
+    tables_copy.wait()
     wo_copy = pltpu.make_async_copy(w_hbm, w_out, wo_sem)
     wo_copy.start()
 
@@ -117,7 +126,7 @@
     def _(c):
         compute(me, c)
 
-    cos, sin = cos_ref[...], sin_ref[...]
+    cos, sin = tables[0], tables[1]
     lane = lax.broadcasted_iota(jnp.int32, (HD, kw), 1)
     source = lax.broadcasted_iota(jnp.int32, (HD, kw), 0)
     pick = (source == (me * kw + lane) // (2 * KV_HEADS) * 2 + lane % 2).astype(jnp.float32)
@@ -290,7 +299,7 @@
     frequency = np.exp(pair * np.float32(-2.0 * math.log(ROPE_BASE) / HD)).astype(np.float32)
     angles = frequency[None, :] * np.arange(length, dtype=np.float32)[:, None]
     sign = np.where(np.arange(HD) % 2 == 0, -1.0, 1.0).astype(np.float32)
-    return np.cos(angles).astype(np.float32), (np.sin(angles) * sign).astype(np.float32)
+    return np.stack([np.cos(angles), np.sin(angles) * sign]).astype(np.float32)
 
 
 def local(arriving, norm_gain, w_query, w_key, w_value, w_out):
@@ -301,18 +310,21 @@
     chunks = 8 if n <= 8 else 2
     pieces = 4 if n <= 8 else 2
     qw, kw, vw = w_query.shape[1], w_key.shape[1], w_value.shape[1]
-    cos, sin = rotary_tables(length)
+    tables = rotary_tables(length)
     vmem = pl.BlockSpec(memory_space=pltpu.VMEM)
-    anywhere = pl.BlockSpec(memory_space=pl.ANY)
+    hbm = pl.BlockSpec(memory_space=pltpu.HBM)
     bf16, f32 = jnp.bfloat16, jnp.float32
     dma = pltpu.SemaphoreType.DMA
     attended, stream = pl.pallas_call(
         functools.partial(layer_kernel, n, chunks, pieces),
         name="layer",
-        out_shape=(jax.ShapeDtypeStruct((rows, full), bf16),) * 2,
-        in_specs=[anywhere, vmem, anywhere, anywhere, anywhere, anywhere, vmem, vmem],
+        out_shape=(pltpu.VMEM((rows, full), bf16),) * 2,
+        in_specs=[hbm] * 7,
         out_specs=(vmem, vmem),
         scratch_shapes=[
+            pltpu.VMEM((n, rows, width), bf16),
+            pltpu.VMEM((n, 1, width), bf16),
+            pltpu.VMEM((2, length, HD), f32),
             pltpu.VMEM((n, n, rows, width), bf16),
             pltpu.VMEM((n, qw + kw + vw, width), bf16),
             pltpu.VMEM((chunks, length // chunks, qw + kw + vw), f32),
@@ -326,6 +338,9 @@
             pltpu.VMEM((qw, full), bf16),
             pltpu.VMEM((n, rows, qw), bf16),
             pltpu.VMEM((2, n, pieces, rows, full // (2 * pieces)), bf16),
+            dma(()),
+            dma(()),
+            dma(()),
             dma((n, 3)),
             dma(()),
             dma((chunks,)),
@@ -341,7 +356,7 @@
     )(
         arriving[0].reshape(n, rows, width),
         norm_gain[0].reshape(n, 1, width),
-        w_query[0], w_key[0], w_value[0], w_out[0], jnp.asarray(cos), jnp.asarray(sin),
+        w_query[0], w_key[0], w_value[0], w_out[0], jnp.asarray(tables),
     )
     return (attended[None], stream[None])
 

time: 268 us -> 266 us (level)
  no operation moved by 1% of the time
where the time goes in v3:
time: 266 us
  Pallas kernels  261 us (98%)
  local copies, waits for them, and re-layouts  4.17 us (2%)
    pallas_call x1, Pallas kernels, local(): pl.pallas_call(functools.partial(layer_kernel, n, chunks, pieces), name='...  261 us

profile of v3, /device:TPU:4, one launch (start us, length us, event | category | flops | bytes accessed | tf_op | source)
XLA Modules:
  0.0 265.7 jit_solution(3138785214870257343)
XLA Ops:
  0.6 0.0 copy-start
  0.6 1.1 copy-done
  1.8 0.0 copy-start.1
  1.8 0.8 copy-done.1
  2.5 260.8 %layer.1 = (bf16[96,8192]{1,0:T(8,128)(2,1)S(1)}, bf16[96,8192]{1,0:T(8,128)(2,1)S(1)}) custom-call(bf16[8,96,1024]{2,1,0:T(8,128)(2,1)} %bitcast.15, bf16[8,1,1024]{2,1,0:T(2,128)(2,1)S(1)} %bitcast.10, bf16[256,8192]{1,0:T(8,128)(2,1)} %bitcast.11, bf16[128,8192]{1,0:T(8,128)(2,1)} %bitcast.13, bf16[128,8192]{1,0:T(8,128)(2,1)} %bitcast.14, ...), custom_call_target="tpu_custom_call" | custom-call | tf_op jit(solution)/shard_map/layer/pallas_call | solution.py:318
  263.4 1.1 copy.11
  264.5 1.1 copy.12
Async XLA Ops:
  0.6 1.1 copy-start
  1.8 0.8 copy-start.1

commit v4 on v3

--- a/solution.py
+++ b/solution.py
@@ -14,7 +14,7 @@
 ROPE_BASE = 500000.0
 NORM_EPS = 1e-05
 MESH = pl.DeviceIdType.MESH
-VMEM_LIMIT = 52000000
+VMEM_LIMIT = 63500000
 
 
 def ring_position(member, n):
@@ -141,8 +141,9 @@
     @pl.loop(0, hops * chunks)
     def _(i):
         hop = i // chunks + 1
-        c = lax.rem(i, chunks)
+        turn = lax.rem(i, chunks)
         last = hop == hops
+        c = jnp.where(last, turn // 2 + lax.rem(turn, 2) * (chunks // 2), turn)
         low = c < chunks // 2
         for way in range(2):
             mine = low if way == 0 else jnp.logical_not(low)
@@ -174,44 +175,51 @@
         for h in range(KV_HEADS):
             sent[h, part] = ordered[h * per_head : (h + 1) * per_head].astype(jnp.bfloat16)
 
-    def kv_copy(step):
+    def kv_copy(part, step):
         other = lax.rem(me + step, n)
         return pltpu.make_async_remote_copy(
-            src_ref=sent.at[other * heads // group_size], dst_ref=got.at[me],
-            send_sem=kv_send.at[step - 1], recv_sem=kv_recv.at[step - 1],
+            src_ref=sent.at[other * heads // group_size, part], dst_ref=got.at[me, part],
+            send_sem=kv_send.at[part, step - 1], recv_sem=kv_recv.at[part, step - 1],
             device_id={"mp": other}, device_id_type=MESH,
         )
 
-    for step in range(1, n):
-        kv_copy(step).start()
+    for part in range(2):
+        for step in range(1, n):
+            kv_copy(part, step).start()
     got[me] = sent[me * heads // group_size]
     for h in range(heads):
         q = acc[:, :, h * HD : (h + 1) * HD].reshape(length, HD) * inverse
         q_ref[:, :, h * HD : (h + 1) * HD] = (
             (q * cos + swap_pairs(q) * sin).reshape(n, rows, HD).astype(jnp.bfloat16)
         )
-    for step in range(1, n):
-        kv_copy(step).wait_recv()
-    for j in range(n):
-        for part in range(2):
+
+    def receive(part, whole):
+        for step in range(1, n):
+            kv_copy(part, step).wait_recv()
+        for j in range(n):
             heads_kv[part, j * per_head : (j + 1) * per_head] = got[j, part].astype(jnp.float32)
-    key_head[...] = heads_kv[0].astype(jnp.bfloat16)
-    value_head[...] = heads_kv[1].astype(jnp.bfloat16)
+        whole[...] = heads_kv[part].astype(jnp.bfloat16)
+
+    receive(0, key_head)
 
     piece_width = running.shape[4]
     scale = 1.0 / math.sqrt(HD)
 
-    def attend(block):
+    def attend(block, ready=None):
         row = lax.broadcasted_iota(jnp.int32, (rows, length), 0) + block * rows
         column = lax.broadcasted_iota(jnp.int32, (rows, length), 1)
+        probs = []
         for h in range(heads):
             q = q_ref[block, :, h * HD : (h + 1) * HD]
             scores = lax.dot_general(q, key_head[...], nn, preferred_element_type=jnp.float32) * scale
             scores = jnp.where(row >= column, scores, -1e30)
             exponent = jnp.exp(scores - jnp.max(scores, axis=1, keepdims=True))
-            probs = (exponent / jnp.sum(exponent, axis=1, keepdims=True)).astype(jnp.bfloat16)
+            probs.append((exponent / jnp.sum(exponent, axis=1, keepdims=True)).astype(jnp.bfloat16))
+        if ready is not None:
+            ready()
+        for h in range(heads):
             context[block, :, h * HD : (h + 1) * HD] = lax.dot_general(
-                probs, value_head[...], nt, preferred_element_type=jnp.float32
+                probs[h], value_head[...], nt, preferred_element_type=jnp.float32
             ).astype(jnp.bfloat16)
 
     def block_of(way, step):
@@ -233,7 +241,7 @@
 
     wo_copy.wait()
     for way in range(2):
-        attend(block_of(way, 0))
+        attend(block_of(way, 0), functools.partial(receive, 1, value_head) if way == 0 else None)
         for piece in range(pieces):
             running[way, 0, piece] = term(way, 0, piece).astype(jnp.bfloat16)
             sum_copy(way, 0, piece).start()
@@ -273,8 +281,9 @@
 
     for c in range(chunks):
         shift_copy(c).wait_send()
-    for step in range(1, n):
-        kv_copy(step).wait_send()
+    for part in range(2):
+        for step in range(1, n):
+            kv_copy(part, step).wait_send()
 
     @pl.loop(0, hops * chunks)
     def _(i):
@@ -347,8 +356,8 @@
             dma((chunks,)),
             dma((2, n // 2, chunks)),
             dma((2, n // 2, chunks)),
-            dma((n - 1,)),
-            dma((n - 1,)),
+            dma((2, n - 1)),
+            dma((2, n - 1)),
             dma((2, n - 1, pieces)),
             dma((2, n - 1, pieces)),
         ],

time: 266 us -> 262 us (0.985)
  no operation moved by 1% of the time
where the time goes in v4:
time: 262 us
  Pallas kernels  259 us (99%)
    pallas_call x1, Pallas kernels, local(): pl.pallas_call(functools.partial(layer_kernel, n, chunks, pieces), name='...  259 us

profile of v4, /device:TPU:4, one launch (start us, length us, event | category | flops | bytes accessed | tf_op | source)
XLA Modules:
  0.0 262.2 jit_solution(13709264291631780239)
XLA Ops:
  0.6 259.3 %layer.1 = (bf16[96,8192]{1,0:T(8,128)(2,1)S(1)}, bf16[96,8192]{1,0:T(8,128)(2,1)S(1)}) custom-call(bf16[8,96,1024]{2,1,0:T(8,128)(2,1)} %bitcast.14, bf16[8,1,1024]{2,1,0:T(2,128)(2,1)} %bitcast.15, bf16[256,8192]{1,0:T(8,128)(2,1)} %bitcast.10, bf16[128,8192]{1,0:T(8,128)(2,1)} %bitcast.12, bf16[128,8192]{1,0:T(8,128)(2,1)} %bitcast.13, ...), custom_call_target="tpu_custom_call" | custom-call | tf_op jit(solution)/shard_map/layer/pallas_call | solution.py:327
  259.9 1.1 copy.11
  261.1 1.1 copy.12

commit v5 on v4

--- a/solution.py
+++ b/solution.py
@@ -169,12 +169,6 @@
     )
     k = acc[:, :, qw : qw + kw].reshape(length, kw) * inverse
     k_rot = (k * k_cos + swap_pairs(k) * k_sin).astype(jnp.bfloat16)
-    v_bf = (acc[:, :, qw + kw :].reshape(length, vw) * inverse).astype(jnp.bfloat16)
-    for part, rotated in enumerate((k_rot, v_bf)):
-        ordered = lax.dot_general(order, rotated, nt, preferred_element_type=jnp.float32)
-        for h in range(KV_HEADS):
-            sent[h, part] = ordered[h * per_head : (h + 1) * per_head].astype(jnp.bfloat16)
-
     def kv_copy(part, step):
         other = lax.rem(me + step, n)
         return pltpu.make_async_remote_copy(
@@ -183,9 +177,15 @@
             device_id={"mp": other}, device_id_type=MESH,
         )
 
-    for part in range(2):
+    def order_and_send(part, channels):
+        ordered = lax.dot_general(order, channels, nt, preferred_element_type=jnp.float32)
+        for h in range(KV_HEADS):
+            sent[h, part] = ordered[h * per_head : (h + 1) * per_head].astype(jnp.bfloat16)
         for step in range(1, n):
             kv_copy(part, step).start()
+
+    order_and_send(0, k_rot)
+    order_and_send(1, (acc[:, :, qw + kw :].reshape(length, vw) * inverse).astype(jnp.bfloat16))
     got[me] = sent[me * heads // group_size]
     for h in range(heads):
         q = acc[:, :, h * HD : (h + 1) * HD].reshape(length, HD) * inverse

time: 262 us -> 262 us (level)
  no operation moved by 1% of the time
where the time goes in v5:
time: 262 us
  Pallas kernels  259 us (99%)
    pallas_call x1, Pallas kernels, local(): pl.pallas_call(functools.partial(layer_kernel, n, chunks, pieces), name='...  259 us

profile of v5, /device:TPU:4, one launch (start us, length us, event | category | flops | bytes accessed | tf_op | source)
XLA Modules:
  0.0 262.2 jit_solution(3461691908761710543)
XLA Ops:
  0.6 259.2 %layer.1 = (bf16[96,8192]{1,0:T(8,128)(2,1)S(1)}, bf16[96,8192]{1,0:T(8,128)(2,1)S(1)}) custom-call(bf16[8,96,1024]{2,1,0:T(8,128)(2,1)} %bitcast.14, bf16[8,1,1024]{2,1,0:T(2,128)(2,1)} %bitcast.15, bf16[256,8192]{1,0:T(8,128)(2,1)} %bitcast.10, bf16[128,8192]{1,0:T(8,128)(2,1)} %bitcast.12, bf16[128,8192]{1,0:T(8,128)(2,1)} %bitcast.13, ...), custom_call_target="tpu_custom_call" | custom-call | tf_op jit(solution)/shard_map/layer/pallas_call | solution.py:327
  259.9 1.1 copy.11
  261.0 1.1 copy.12
